TPU v7x, 32 devices: a whole 2x2x4 slice. The times are simulated.
32 devices in a mesh: tm: 4 (over z), mem: 4 (over y, x), tile: 2 (over core).
Axes of the slice: x: 2, y: 2, z: 4, core: 2. Of those that a mesh axis runs over, the one named last changes fastest.
Arguments:
- control: float32 [40, 2, 8, 256], P('mem', None, 'tile'), may hold values from -6 to 6
- vertical_modes: float32 [64, 2], replicated, may hold values from -4 to 4
- mode_counts: int32 [8], P('tile'), may hold values from 1 to 2, as said below
- perturbations: bfloat16 [40, 8, 64, 8, 256], P('mem', 'tm', None, 'tile'), may hold values from -6 to 6
- slot_index: int32 [12], P('tm'), may hold values from 0 to 7, as said below
- blend_weight: float32 [12], P('tm'), may hold values from 0 to 1
Outputs:
- increment: float32 [12, 64, 8, 256], P('tm', None, 'tile')
Inputs may be any that keep to these rules, and one draw needn't show every extreme that they name: slot_index[w] // 2 == w // 3. `mode_counts`: both ends of the range occur.
All inputs are finite; a program needn't handle non-finite values.
Results may differ from a plain program's by a relative error of at most 0.0003.
Values sent between devices are 32-bit elements; how exact they have to be, the bound alone decides.
A program may use at most 64 MiB of HBM per device.

v0:
```python
import math

import jax
import jax.numpy as jnp
from jax import lax
from jax.sharding import PartitionSpec as P

VM = 2
SMOOTH = 4


diffusion = 0.24


def padded_2(cells, sides, width):
    for axis, dim in sides:
        count = lax.axis_size(axis)
        head = lax.slice_in_dim(cells, 0, width, axis=dim)
        tail = lax.slice_in_dim(cells, cells.shape[dim] - width, cells.shape[dim], axis=dim)
        cells = jnp.concatenate(
            [
                lax.ppermute(tail, axis, [(i, (i + 1) % count) for i in range(count)]),
                cells,
                lax.ppermute(head, axis, [((i + 1) % count, i) for i in range(count)]),
            ],
            axis=dim,
        )
    return cells


def prefix(part, axis, combine, identity):
    place = lax.axis_index(axis)
    gathered = lax.all_gather(part, axis)
    state = jnp.zeros_like(part) + jnp.asarray(identity, part.dtype)

    def one(lap, state):
        return combine(state, lax.dynamic_index_in_dim(gathered, lap, 0, False))

    return lax.fori_loop(0, place, one, state)


def relax_local(padded):
    center = padded[:, :, 1:-1]
    neighbours = padded[:, :, 2:] + padded[:, :, :-2]
    bordered = jnp.pad(center, ((0, 0), (0, 0), (0, 0), (1, 1)))
    lateral = bordered[:, :, :, 2:] + bordered[:, :, :, :-2]
    return center + diffusion * (neighbours + lateral - 4.0 * center)


def add_terms(earlier, later):
    return earlier + later


def per_device(control, vertical_modes, mode_counts, perturbations, slot_index, blend_weight):
    field = control
    for repeat in range(SMOOTH):
        field = relax_local(padded_2(field, (("tile", 2),), 1))
    members = perturbations.shape[0]
    slot_count = perturbations.shape[1]
    levels = perturbations.shape[2]
    localized = jnp.zeros((members, levels) + field.shape[2:], jnp.float32)
    for mode_index in range(VM):
        keep_mode = (mode_index < mode_counts).astype(jnp.float32)
        masked = keep_mode[None, :, None] * field[:, mode_index]
        localized = localized + vertical_modes[:, mode_index][None, :, None, None] * masked[:, None]
    partial_sum = jnp.sum(localized[:, None] * perturbations.astype(jnp.float32), axis=0)
    norm_factor = 1.0 / math.sqrt(members * lax.axis_size("mem") - 1)
    member_total = lax.psum_scatter(partial_sum, "mem", scatter_dimension=1, tiled=True)
    running = jnp.cumsum(member_total * norm_factor, axis=0)
    earlier = prefix(running[-1], "tm", add_terms, jnp.zeros_like(running[-1]))
    extended = jnp.concatenate([earlier[None], earlier[None] + running], axis=0)
    local_slot = slot_index - lax.axis_index("tm") * slot_count
    positions = jnp.arange(slot_count + 1, dtype=jnp.int32)[None, :]
    weight = blend_weight[:, None]
    table = weight * (positions == local_slot[:, None] + 1).astype(jnp.float32)
    table = table + (1.0 - weight) * (positions == local_slot[:, None]).astype(jnp.float32)
    blended = jnp.einsum("we,elxy->wlxy", table, extended, precision=lax.Precision.HIGHEST)
    blended = lax.all_gather(blended, "mem", axis=1, tiled=True)
    return blended


def solution(mesh):
    placed = (
        P("mem", None, "tile", None),
        P(),
        P("tile"),
        P("mem", "tm", None, "tile", None),
        P("tm"),
        P("tm"),
    )
    return jax.shard_map(
        per_device,
        mesh=mesh,
        in_specs=placed,
        out_specs=P("tm", None, "tile", None),
        check_vma=False,
    )
```

profile of v0, /device:TPU:24, one launch (start us, length us, event | category | flops | bytes accessed | tf_op | source)
XLA Modules:
  0.0 101.3 jit_solution(3416503850323583249)
XLA Ops:
  6.5 0.0 all-reduce.7.cloned.1.call-start
  6.5 1.1 %fusion.45 = (f32[10,2,1,256]{3,2,1,0:T(1,128)S(1)}, f32[10,2,1,256]{3,2,1,0:T(1,128)S(1)}) fusion(f32[10,2,4,256]{3,2,1,0:T(4,128)} %param.8), kind=kLoop, calls=%fused_computation.79 | loop fusion | bytes 81920 | tf_op jit(solution)/shard_map/slice | solution.py:18
  7.7 0.1 collective-permute-start
  7.7 0.5 collective-permute-start.1
  8.2 0.7 collective-permute-done
  8.9 0.2 collective-permute-done.1
  9.1 1.3 %fusion.9 = f32[10,2,4,256]{3,2,1,0:T(4,128)S(1)} fusion(f32[10,2,4,256]{3,2,1,0:T(4,128)} %param.8, f32[10,2,1,256]{3,2,1,0:T(1,128)S(1)} %collective-permute-done.1, f32[10,2,1,256]{3,2,1,0:T(1,128)S(1)} %collective-permute-done), kind=kLoop, calls=%fused_computation.22 | loop fusion | flops 184320 | bytes 204800 | tf_op jit(solution)/shard_map/add | solution.py:47
  10.5 0.4 collective-permute-start.2
  10.9 0.2 collective-permute-start.3
  11.0 0.7 collective-permute-done.2
  11.7 0.3 collective-permute-done.3
  12.1 0.2 fusion.14
  12.3 0.2 collective-permute-start.4
  12.5 0.3 collective-permute-start.5
  12.8 0.8 slice_bitcast_fusion.1
  13.6 0.0 collective-permute-done.4
  13.6 0.1 collective-permute-done.5
  13.7 0.2 fusion.19
  13.9 0.4 collective-permute-start.6
  14.3 0.2 collective-permute-start.7
  14.5 0.7 compare_convert_fusion.1
  15.1 0.0 collective-permute-done.6
  15.1 0.3 collective-permute-done.7
  15.5 0.2 fusion.24
  15.7 0.1 fusion.30
  15.7 0.8 multiply_add_fusion
  16.5 0.0 copy-start.3
  16.5 0.0 copy-start.1
  16.5 0.0 copy-start.2
  16.6 1.6 %multiply_reduce_fusion = f32[2,64,4,256]{3,2,1,0:T(4,128)S(1)} fusion(bf16[10,2,64,4,256]{4,3,2,1,0:T(4,128)(2,1)S(1)} %copy-done, f32[10,64,4,256]{3,2,1,0:T(4,128)S(1)} %multiply_add_fusion), kind=kLoop, calls=%fused_computation.3 | loop fusion | flops 3801088 | bytes 5767168 | tf_op jit(solution)/shard_map/reduce_sum | solution.py:66
  18.2 0.8 copy.9
  19.0 0.0 all-reduce.7.cloned.1.call-update
  19.0 0.6 dynamic-slice
  20.3 45.2 %all-reduce.7.cloned.1.call-done = f32[2,64,4,256]{3,2,0,1:T(4,128)} async-done(((f32[2,64,4,256]{3,2,0,1:T(4,128)}), f32[2,64,4,256]{3,2,0,1:T(4,128)}) %all-reduce.7.cloned.1.call-update) | async-done | bytes 524304
  65.5 0.9 constant_dynamic-slice_fusion.1
  66.4 0.1 copy_multiply_fusion
  66.5 0.3 reduce_window_sum.11
  66.8 0.1 slice.132
  66.9 14.3 %all_gather.6 = f32[4,16,4,256]{3,1,2,0:T(8,128)S(1)} all-gather(f32[1,16,4,256]{3,1,2,0:T(8,128)S(1)} %copy.11), channel_id=1, replica_groups=mesh['tm'=4,'mem'=4,'tile'=2] {'tm'}, dimensions={0}, use_global_device_ids=true | all-gather | bytes 327680 | tf_op jit(solution)/shard_map/all_gather | solution.py:33
  81.2 0.4 while.10
  81.2 0.1 fusion.47
  81.3 0.1 fusion.47
  81.5 0.1 fusion.47
  81.6 0.1 broadcast_add_fusion
  81.7 0.6 fusion.1
  82.3 0.1 copy.13
  82.4 11.0 %all_gather.7 = f32[3,64,4,256]{3,2,0,1:T(4,128)S(1)} all-gather(f32[3,16,4,256]{3,2,0,1:T(4,128)S(1)} %copy.13), channel_id=1, replica_groups=mesh['tm'=4,'mem'=4,'tile'=2] {'mem'}, dimensions={1}, use_global_device_ids=true | all-gather | bytes 983040 | tf_op jit(solution)/shard_map/all_gather | solution.py:78
  93.4 1.0 %copy.14 = f32[3,64,4,256]{3,2,1,0:T(4,128)} copy(f32[3,64,4,256]{3,2,0,1:T(4,128)S(1)} %all_gather.7) | data formatting | bytes 1572864 | tf_op jit(solution)/shard_map/all_gather | solution.py:78
  (16 shorter events, 0.2 us)
Async XLA Ops:
  6.5 10.0 %copy-start = (bf16[10,2,64,4,256]{4,3,2,1,0:T(4,128)(2,1)S(1)}, bf16[10,2,64,4,256]{4,3,2,1,0:T(4,128)(2,1)}, u32[]{:S(2)}) copy-start(bf16[10,2,64,4,256]{4,3,2,1,0:T(4,128)(2,1)} %param.11) | copy-start | bytes 7864324
  6.5 59.0 %all-reduce.7.cloned.1.call-start = ((), (), s32[]{:S(2)}) async-start(), calls=%async_computation | async-start | bytes 1048576
  7.7 1.3 %collective-permute-start = (f32[10,2,1,256]{3,2,1,0:T(1,128)S(1)}, f32[10,2,1,256]{3,2,1,0:T(1,128)S(1)}, u32[]{:S(2)}, u32[]{:S(2)}) collective-permute-start(f32[10,2,1,256]{3,2,1,0:T(1,128)S(1)} %get-tuple-element.55), channel_id=1, source_target_pairs={{1,0},{0,1},{3,2},{2,3},{5,4},{4,5},{7,6},{6,7},{9,8},{8,9},{11,10... | collective-permute-start | bytes 61448 | tf_op jit(solution)/shard_map/ppermute | solution.py:24
  7.7 1.3 %collective-permute-start.1 = (f32[10,2,1,256]{3,2,1,0:T(1,128)S(1)}, f32[10,2,1,256]{3,2,1,0:T(1,128)S(1)}, u32[]{:S(2)}, u32[]{:S(2)}) collective-permute-start(f32[10,2,1,256]{3,2,1,0:T(1,128)S(1)} %get-tuple-element.56), channel_id=1, source_target_pairs={{0,1},{1,0},{2,3},{3,2},{4,5},{5,4},{6,7},{7,6},{8,9},{9,8},{10,11... | collective-permute-start | bytes 61448 | tf_op jit(solution)/shard_map/ppermute | solution.py:22
  10.5 1.3 %collective-permute-start.2 = (f32[10,2,1,256]{3,2,1,0:T(1,128)S(1)}, f32[10,2,1,256]{3,2,1,0:T(1,128)S(1)}, u32[]{:S(2)}, u32[]{:S(2)}) collective-permute-start(f32[10,2,1,256]{3,2,1,0:T(1,128)S(1)} %get-tuple-element.53), channel_id=1, source_target_pairs={{1,0},{0,1},{3,2},{2,3},{5,4},{4,5},{7,6},{6,7},{9,8},{8,9},{11,10... | collective-permute-start | bytes 61448 | tf_op jit(solution)/shard_map/ppermute | solution.py:24
  10.9 1.2 %collective-permute-start.3 = (f32[10,2,1,256]{3,2,1,0:T(1,128)S(1)}, f32[10,2,1,256]{3,2,1,0:T(1,128)S(1)}, u32[]{:S(2)}, u32[]{:S(2)}) collective-permute-start(f32[10,2,1,256]{3,2,1,0:T(1,128)S(1)} %get-tuple-element.54), channel_id=1, source_target_pairs={{0,1},{1,0},{2,3},{3,2},{4,5},{5,4},{6,7},{7,6},{8,9},{9,8},{10,11... | collective-permute-start | bytes 61448 | tf_op jit(solution)/shard_map/ppermute | solution.py:22
  12.3 1.3 %collective-permute-start.4 = (f32[10,2,1,256]{3,2,1,0:T(1,128)S(1)}, f32[10,2,1,256]{3,2,1,0:T(1,128)S(1)}, u32[]{:S(2)}, u32[]{:S(2)}) collective-permute-start(f32[10,2,1,256]{3,2,1,0:T(1,128)S(1)} %get-tuple-element.51), channel_id=1, source_target_pairs={{1,0},{0,1},{3,2},{2,3},{5,4},{4,5},{7,6},{6,7},{9,8},{8,9},{11,10... | collective-permute-start | bytes 61448 | tf_op jit(solution)/shard_map/ppermute | solution.py:24
  12.5 1.2 %collective-permute-start.5 = (f32[10,2,1,256]{3,2,1,0:T(1,128)S(1)}, f32[10,2,1,256]{3,2,1,0:T(1,128)S(1)}, u32[]{:S(2)}, u32[]{:S(2)}) collective-permute-start(f32[10,2,1,256]{3,2,1,0:T(1,128)S(1)} %get-tuple-element.52), channel_id=1, source_target_pairs={{0,1},{1,0},{2,3},{3,2},{4,5},{5,4},{6,7},{7,6},{8,9},{9,8},{10,11... | collective-permute-start | bytes 61448 | tf_op jit(solution)/shard_map/ppermute | solution.py:22
  13.9 1.3 %collective-permute-start.6 = (f32[10,2,1,256]{3,2,1,0:T(1,128)S(1)}, f32[10,2,1,256]{3,2,1,0:T(1,128)S(1)}, u32[]{:S(2)}, u32[]{:S(2)}) collective-permute-start(f32[10,2,1,256]{3,2,1,0:T(1,128)S(1)} %get-tuple-element.49), channel_id=1, source_target_pairs={{1,0},{0,1},{3,2},{2,3},{5,4},{4,5},{7,6},{6,7},{9,8},{8,9},{11,10... | collective-permute-start | bytes 61448 | tf_op jit(solution)/shard_map/ppermute | solution.py:24
  14.3 1.2 %collective-permute-start.7 = (f32[10,2,1,256]{3,2,1,0:T(1,128)S(1)}, f32[10,2,1,256]{3,2,1,0:T(1,128)S(1)}, u32[]{:S(2)}, u32[]{:S(2)}) collective-permute-start(f32[10,2,1,256]{3,2,1,0:T(1,128)S(1)} %get-tuple-element.50), channel_id=1, source_target_pairs={{0,1},{1,0},{2,3},{3,2},{4,5},{5,4},{6,7},{7,6},{8,9},{9,8},{10,11... | collective-permute-start | bytes 61448 | tf_op jit(solution)/shard_map/ppermute | solution.py:22
  16.5 2.5 %copy-start.3 = (u32[32]{0:T(128)S(1)}, u32[32]{0:T(128)}, u32[]{:S(2)}) copy-start(u32[32]{0:T(128)} %constant.52) | copy-start | bytes 388
  16.5 3.8 %copy-start.1 = (f32[3]{0:T(128)S(1)}, f32[3]{0:T(128)}, u32[]{:S(2)}) copy-start(f32[3]{0:T(128)} %param.13) | copy-start | bytes 40
  16.5 3.8 %copy-start.2 = (s32[3]{0:T(128)S(1)}, s32[3]{0:T(128)}, u32[]{:S(2)}) copy-start(s32[3]{0:T(128)} %param.12) | copy-start | bytes 40
Sparse Core Ops, SparseCore 0:
  19.1 46.3 all-reduce.6
where the time goes:
time: 103 us; the launch traced here: 101 us
  waiting for transfers between devices  47.5 us (46%)
  blocking collectives  25.3 us (25%)
  between operations  14.2 us (14%)
  other arithmetic  5.67 us (6%)
  local copies, waits for them, and re-layouts  5.59 us (5%)
  starting transfers between devices  2.3 us (2%)
    unnamed x2, waiting for transfers between devices  45.2 us
    all_gather x1, blocking collectives, prefix(): gathered = lax.all_gather(part, axis)  14.3 us
    all_gather x1, blocking collectives, per_device(): blended = lax.all_gather(blended, 'mem', axis=1, tiled=True)  11 us
  transfers between devices with their start and end apart: 9, of which 7 were waited for; matrix products, arithmetic and copies ran while one was open for 2% of the time, Pallas kernels for 0%

commit v1 on v0

v1 whole, which is shorter than its diff:
```python
import functools
import math

import jax
import jax.numpy as jnp
from jax import lax
from jax.experimental import pallas as pl
from jax.experimental.pallas import tpu as pltpu
from jax.sharding import PartitionSpec as P

SMOOTH = 4
LANES = 128
MESH = pl.DeviceIdType.MESH

diffusion = 0.24


def kernel(dims, control, perturbations, modes, counts, ext, own, near, pert, smooth, part,
           first_a, first_b, mid_a, mid_b, second_a, second_b, passing,
           load_sem, pert_sem, halo_send, halo_recv, rs_send, rs_recv, z_send, z_recv, ag_send, ag_recv):
    members, slots, modes_n, nx, halves, outer, inner, rows, tiles, steps_tm, norm = dims
    tm = lax.axis_index("tm")
    mem = lax.axis_index("mem")
    tile = lax.axis_index("tile")
    jy, ix = mem // inner, mem % inner
    level_rows = nx * halves
    part_levels = rows // level_rows

    def inner_peer(d):
        return (ix + d) % inner

    def outer_peer(d):
        return (jy + d) % outer

    def at(j, i):
        return {"mem": j * inner + i}

    load_own = pltpu.make_async_copy(control, own, load_sem)
    load_own.start()
    order = []
    for d in range(1, inner):
        order += [(0, outer_peer(e), inner_peer(d)) for e in range(1, outer + 1)]
    for e in range(1, outer):
        order += [(1, outer_peer(e), inner_peer(d)) for d in range(1, inner + 1)]
    sent = len(order)
    order += [(0, outer_peer(e), ix) for e in range(1, outer + 1)]
    order += [(1, jy, inner_peer(d)) for d in range(1, inner + 1)]
    loads = []
    for n, (p, j, i) in enumerate(order):
        copy = pltpu.make_async_copy(
            perturbations.at[:, :, j, i, p], pert.at[:, :, j, i, p], pert_sem.at[n])
        copy.start()
        loads.append(copy)

    barrier = pltpu.get_barrier_semaphore()
    tile_offsets = sorted({1 % tiles, (tiles - 1) % tiles} - {0})
    expected = len(tile_offsets) + (inner - 1) + (outer - 1)
    for d in tile_offsets:
        pl.semaphore_signal(barrier, inc=1, device_id={"tile": (tile + d) % tiles}, device_id_type=MESH)
    for d in range(1, inner):
        pl.semaphore_signal(barrier, inc=1, device_id=at(jy, inner_peer(d)), device_id_type=MESH)
    for e in range(1, outer):
        pl.semaphore_signal(barrier, inc=1, device_id=at(outer_peer(e), ix), device_id_type=MESH)

    @pl.when(tm > 0)
    def _():
        pl.semaphore_signal(barrier, inc=1, device_id={"tm": tm - 1}, device_id_type=MESH)

    @pl.when(tm < steps_tm - 1)
    def _():
        pl.semaphore_signal(barrier, inc=1, device_id={"tm": tm + 1}, device_id_type=MESH)

    chain_peers = jnp.where(tm > 0, 1, 0) + jnp.where(tm < steps_tm - 1, 1, 0)
    pl.semaphore_wait(barrier, expected + chain_peers)

    load_own.wait()
    halos = []
    for n, d in enumerate(tile_offsets):
        copy = pltpu.make_async_remote_copy(
            src_ref=own, dst_ref=near.at[n], send_sem=halo_send.at[n], recv_sem=halo_recv.at[n],
            device_id={"tile": (tile + d) % tiles}, device_id_type=MESH)
        copy.start()
        halos.append(copy)
    for copy in halos:
        copy.wait_recv()

    row = lax.broadcasted_iota(jnp.int32, (1, level_rows, LANES), 1)
    lane = lax.broadcasted_iota(jnp.int32, (1, level_rows, LANES), 2)
    lon, half = row % nx, row // nx
    first_lon, last_lon = lon == 0, lon == nx - 1
    first_lane, last_lane = lane == 0, lane == LANES - 1
    has_next, has_prev = half < halves - 1, half > 0
    back = level_rows - 1

    def relax(left, v, right):
        east = jnp.where(last_lon, pltpu.roll(right, nx - 1, 1), pltpu.roll(v, back, 1))
        west = jnp.where(first_lon, pltpu.roll(left, level_rows - (nx - 1), 1), pltpu.roll(v, 1, 1))
        up = pltpu.roll(v, LANES - 1, 2)
        up_next = jnp.where(has_next, pltpu.roll(up, level_rows - nx, 1), 0.0)
        down = pltpu.roll(v, 1, 2)
        down_next = jnp.where(has_prev, pltpu.roll(down, nx, 1), 0.0)
        lateral = jnp.where(last_lane, up_next, up) + jnp.where(first_lane, down_next, down)
        return v + diffusion * (east + west + lateral - 4.0 * v)

    count = jnp.zeros((1, level_rows, LANES), jnp.int32)
    for x in range(nx):
        count = jnp.where(lon == x, counts[x], count)

    fields = own.shape[0]
    batch = fields // 2 if fields % 2 == 0 and (fields // 2) % modes_n == 0 else fields

    def smooth_batch(b, carry):
        span = pl.ds(b * batch, batch)
        c = own[span]
        if tiles == 1:
            for _ in range(SMOOTH):
                c = relax(c, c, c)
        elif tiles == 2:
            o = near[0, span]
            for s in range(SMOOTH):
                c, o = relax(o, c, o), (relax(c, o, c) if s < SMOOTH - 1 else o)
        else:
            left, right = near[0, span], near[1, span]
            for s in range(SMOOTH):
                new = relax(left, c, right)
                if s < SMOOTH - 1:
                    left, right = relax(left, left, c), relax(c, right, right)
                c = new
        mode = lax.broadcasted_iota(jnp.int32, (batch, level_rows, LANES), 0) % modes_n
        smooth[span] = jnp.where(mode < count, c * norm, 0.0)
        return carry

    lax.fori_loop(0, fields // batch, smooth_batch, 0)

    pair = 2 * level_rows

    def block(p, j, i):
        base = ((j * inner + i) * 2 + p) * part_levels

        def body(u, carry):
            for t in range(slots):
                acc = [[None] * 2 for _ in range(modes_n)]
                for k in range(members):
                    x = pert[k, t, j, i, p, pl.ds(pl.multiple_of(u * pair, pair), pair), :].astype(jnp.float32)
                    for m in range(modes_n):
                        s = smooth[k * modes_n + m]
                        for v in range(2):
                            term = s * x[v * level_rows:(v + 1) * level_rows]
                            acc[m][v] = term if k == 0 else acc[m][v] + term
                for v in range(2):
                    total = modes[0, base + 2 * u + v] * acc[0][v]
                    for m in range(1, modes_n):
                        total = total + modes[m, base + 2 * u + v] * acc[m][v]
                    part[p, t, j, i, pl.ds(pl.multiple_of(u * pair + v * level_rows, level_rows), level_rows), :] = total
            return carry

        lax.fori_loop(0, rows // pair, body, 0)

    def remote(src, dst, send, recv, to):
        return pltpu.make_async_remote_copy(
            src_ref=src, dst_ref=dst, send_sem=send, recv_sem=recv, device_id=to, device_id_type=MESH)

    steps_in, steps_out = range(1, inner), range(1, outer)
    n_in = inner - 1
    rs1a = [remote(part.at[0, :, :, inner_peer(d)], first_a.at[d - 1],
                   rs_send.at[0, d - 1], rs_recv.at[0, d - 1], at(jy, inner_peer(d))) for d in steps_in]
    rs1b = [remote(part.at[1, :, outer_peer(e)], first_b.at[e - 1],
                   rs_send.at[1, e - 1], rs_recv.at[1, e - 1], at(outer_peer(e), ix)) for e in steps_out]
    rs2a = [remote(mid_a.at[e - 1], second_a.at[e - 1],
                   rs_send.at[2, e - 1], rs_recv.at[2, e - 1], at(outer_peer(e), ix)) for e in steps_out]
    rs2b = [remote(mid_b.at[d - 1], second_b.at[d - 1],
                   rs_send.at[3, d - 1], rs_recv.at[3, d - 1], at(jy, inner_peer(d))) for d in steps_in]

    n = 0
    for copy in rs1a:
        for _ in range(outer):
            loads[n].wait()
            block(*order[n])
            n += 1
        copy.start()
    for copy in rs1b:
        for _ in range(inner):
            loads[n].wait()
            block(*order[n])
            n += 1
        copy.start()
    while n < len(order):
        loads[n].wait()
        block(*order[n])
        n += 1

    for copy in rs1a:
        copy.wait_recv()
    for e, copy in zip(steps_out, rs2a):
        total = part[0, :, outer_peer(e), ix]
        for d in steps_in:
            total = total + first_a[d - 1, :, outer_peer(e)]
        mid_a[e - 1] = total
        copy.start()
    for copy in rs1b:
        copy.wait_recv()
    for d, copy in zip(steps_in, rs2b):
        total = part[1, :, jy, inner_peer(d)]
        for e in steps_out:
            total = total + first_b[e - 1, :, inner_peer(d)]
        mid_b[d - 1] = total
        copy.start()

    def gathers(unit, row0, p):
        sends, relays = [], []

        def move(j, i, to, sem):
            ref = ext.at[pl.ds(unit, slots) if unit else pl.ds(0, 1), j, i, p]
            return remote(ref, ref, ag_send.at[row0, p, sem], ag_recv.at[row0, p, sem], to)

        sem = 0
        for d in steps_in:
            sends.append(("in", d, move(jy, ix, at(jy, inner_peer(d)), sem)))
            sem += 1
        for e in steps_out:
            sends.append(("out", e, move(jy, ix, at(outer_peer(e), ix), sem)))
            sem += 1
        if p == 0:
            for d in steps_in:
                for e in steps_out:
                    relays.append((d, move(jy, inner_peer(inner - d), at(outer_peer(e), ix), sem)))
                    sem += 1
        else:
            for e in steps_out:
                for d in steps_in:
                    relays.append((e, move(outer_peer(outer - e), ix, at(jy, inner_peer(d)), sem)))
                    sem += 1
        return sends, relays

    slot_gathers = [gathers(1, 0, p) for p in range(2)]
    early_gathers = [gathers(0, 1, p) for p in range(2)]

    def start_gather(g):
        for _, _, copy in g[0]:
            copy.start()

    def relay_gather(g, p):
        kind = "in" if p == 0 else "out"
        for name, d, copy in g[0]:
            if name == kind:
                copy.wait_recv()
                for dd, forward in g[1]:
                    if dd == d:
                        forward.start()

    def finish_gather(g, p):
        kind = "in" if p == 0 else "out"
        for name, _, copy in g[0]:
            if name != kind:
                copy.wait_recv()
        for _, forward in g[1]:
            forward.wait_recv()
        for _, _, copy in g[0]:
            copy.wait_send()
        for _, forward in g[1]:
            forward.wait_send()

    chain = [remote(passing.at[p], ext.at[0, jy, ix, p], z_send.at[p], z_recv.at[p], {"tm": tm + 1})
             for p in range(2)]

    def add_slots(p):
        total = ext[1, jy, ix, p]
        for t in range(1, slots):
            total = total + ext[1 + t, jy, ix, p]
        return total

    def own_total(p):
        if p == 0:
            total = part[0, :, jy, ix]
            for d in steps_in:
                total = total + first_a[d - 1, :, jy]
            for copy in rs2a:
                copy.wait_recv()
            for e in steps_out:
                total = total + second_a[e - 1]
        else:
            total = part[1, :, jy, ix]
            for e in steps_out:
                total = total + first_b[e - 1, :, ix]
            for copy in rs2b:
                copy.wait_recv()
            for d in steps_in:
                total = total + second_b[d - 1]
        ext[pl.ds(1, slots), jy, ix, p] = total

    for p in range(2):
        own_total(p)

        @pl.when(tm == 0)
        def _():
            ext[0, jy, ix, p] = jnp.zeros(ext.shape[4:], jnp.float32)
            if steps_tm > 1:
                passing[p] = add_slots(p)
                chain[p].start()

        start_gather(slot_gathers[p])

    def earlier():
        for p in range(2):
            @pl.when(tm > 0)
            def _():
                chain[p].wait_recv()

                @pl.when(tm < steps_tm - 1)
                def _():
                    passing[p] = ext[0, jy, ix, p] + add_slots(p)
                    chain[p].start()

            start_gather(early_gathers[p])

    def relays():
        for p in range(2):
            relay_gather(slot_gathers[p], p)

    @pl.when(tm <= 1)
    def _():
        earlier()
        relays()

    @pl.when(tm > 1)
    def _():
        relays()
        earlier()

    for p in range(2):
        relay_gather(early_gathers[p], p)
    for p in range(2):
        finish_gather(slot_gathers[p], p)
    for p in range(2):
        finish_gather(early_gathers[p], p)

    @pl.when(tm < steps_tm - 1)
    def _():
        for p in range(2):
            chain[p].wait_send()

    for copy in halos + rs1a + rs1b + rs2a + rs2b:
        copy.wait_send()


def rows_view(x, nx, gy):
    lead = x.shape[:-2]
    x = x.reshape(lead + (nx, gy // LANES, LANES))
    x = jnp.swapaxes(x, -3, -2)
    return x


def per_device(control, vertical_modes, mode_counts, perturbations, slot_index, blend_weight):
    members, slots, levels, nx, gy = perturbations.shape
    modes_n = control.shape[1]
    halves = gy // LANES
    level_rows = nx * halves
    tiles, n_mem, steps_tm = lax.axis_size("tile"), lax.axis_size("mem"), lax.axis_size("tm")
    inner = 2 if n_mem % 2 == 0 else 1
    outer = n_mem // inner
    rows = levels // (n_mem * 2) * level_rows
    assert nx >= SMOOTH and level_rows == 8 and rows % 16 == 0
    norm = 1.0 / math.sqrt(members * n_mem - 1)
    fields = members * modes_n
    c = rows_view(control, nx, gy).reshape(fields, level_rows, LANES)
    q = rows_view(perturbations, nx, gy).reshape(members, slots, outer, inner, 2, rows, LANES)
    dims = (members, slots, modes_n, nx, halves, outer, inner, rows, tiles, steps_tm, norm)
    f32 = jnp.float32
    n_in, n_out = max(inner - 1, 1), max(outer - 1, 1)
    n_gather = max(inner - 1 + outer - 1 + (inner - 1) * (outer - 1), 1)
    dma = pltpu.SemaphoreType.DMA
    ext = pl.pallas_call(
        functools.partial(kernel, dims),
        out_shape=jax.ShapeDtypeStruct((slots + 1, outer, inner, 2, rows, LANES), f32),
        in_specs=[
            pl.BlockSpec(memory_space=pl.ANY),
            pl.BlockSpec(memory_space=pl.ANY),
            pl.BlockSpec(memory_space=pltpu.SMEM),
            pl.BlockSpec(memory_space=pltpu.SMEM),
        ],
        out_specs=pl.BlockSpec(memory_space=pltpu.VMEM),
        scratch_shapes=[
            pltpu.VMEM((fields, level_rows, LANES), f32),
            pltpu.VMEM((2, fields, level_rows, LANES), f32),
            pltpu.VMEM(q.shape, q.dtype),
            pltpu.VMEM((fields, level_rows, LANES), f32),
            pltpu.VMEM((2, slots, outer, inner, rows, LANES), f32),
            pltpu.VMEM((n_in, slots, outer, rows, LANES), f32),
            pltpu.VMEM((n_out, slots, inner, rows, LANES), f32),
            pltpu.VMEM((n_out, slots, rows, LANES), f32),
            pltpu.VMEM((n_in, slots, rows, LANES), f32),
            pltpu.VMEM((n_out, slots, rows, LANES), f32),
            pltpu.VMEM((n_in, slots, rows, LANES), f32),
            pltpu.VMEM((2, rows, LANES), f32),
            dma,
            dma((2 * n_mem,)),
            dma((2,)),
            dma((2,)),
            dma((4, max(n_in, n_out))),
            dma((4, max(n_in, n_out))),
            dma((2,)),
            dma((2,)),
            dma((2, 2, n_gather)),
            dma((2, 2, n_gather)),
        ],
        compiler_params=pltpu.CompilerParams(collective_id=0, has_side_effects=True),
    )(c, q, vertical_modes.T, mode_counts)
    ext = ext.reshape(slots + 1, levels, halves, nx, LANES)
    ext = jnp.swapaxes(ext, 2, 3).reshape(slots + 1, levels, nx, gy)
    local = slot_index - lax.axis_index("tm") * slots
    out = ext[0][None]
    for t in range(slots):
        share = jnp.where(local > t, 1.0, jnp.where(local == t, blend_weight, 0.0))
        out = out + share[:, None, None, None] * ext[1 + t][None]
    return out


def solution(mesh):
    placed = (
        P("mem", None, "tile", None),
        P(),
        P("tile"),
        P("mem", "tm", None, "tile", None),
        P("tm"),
        P("tm"),
    )
    return jax.shard_map(
        per_device,
        mesh=mesh,
        in_specs=placed,
        out_specs=P("tm", None, "tile", None),
        check_vma=False,
    )
```

time: 103 us -> 30.4 us (0.30); the launches traced: 101 us -> 30.2 us
  waiting for transfers between devices: 47.5 us -> 0 us
  Pallas kernels: 0 us -> 27.7 us
  blocking collectives: 25.3 us -> 0 us
  between operations: 14.2 us -> 0.04 us
  other arithmetic: 5.67 us -> 1.16 us
  local copies, waits for them, and re-layouts: 5.59 us -> 1.25 us
  starting transfers between devices: 2.3 us -> 0 us
    unnamed x2 -> x0, waiting for transfers between devices: 45.2 us -> none
    pallas_call x0 -> x1, Pallas kernels: none -> 27.7 us  [per_device(): pl.pallas_call(functools.partial(kernel, dims), out_shape=jax.ShapeDtypeS...]
    all_gather x2 -> x0, blocking collectives: 25.3 us -> none  [the longest x1 14.3 us: prefix(): gathered = lax.all_gather(part, axis)]
    ppermute x8 -> x0, waiting for transfers between devices: 2.32 us -> none  [the longest x4 1.38 us: padded_2(): lax.ppermute(head, axis, [((i + 1) % count, i) for i in range(count)])]
    ppermute x8 -> x0, starting transfers between devices: 2.29 us -> none  [the longest x4 1.17 us: padded_2(): lax.ppermute(tail, axis, [(i, (i + 1) % count) for i in range(count)])]
    add x10 -> x1, other arithmetic: 2.97 us -> 1.15 us  [per_device(): out = out + share[:, None, None, None] * ext[1 + t][None]]
    reduce_sum x1 -> x0, other arithmetic: 1.6 us -> none  [per_device(): jnp.sum(localized[:, None] * perturbations.astype(jnp.float32), axis=0)]
    unnamed x10 -> x4, local copies, waits for them, and re-layouts: 1.54 us -> 0.01 us
  transfers between devices with their start and end apart: 9 -> 0, of which waited for: 7 -> 0; matrix products, arithmetic and copies ran while one was open for 2% -> 0% of each run, Pallas kernels for 0% -> 0%
where the time goes in v1:
time: 30.4 us; the launch traced here: 30.2 us
  Pallas kernels  27.7 us (91%)
  local copies, waits for them, and re-layouts  1.25 us (4%)
  other arithmetic  1.16 us (4%)
    pallas_call x1, Pallas kernels, per_device(): pl.pallas_call(functools.partial(kernel, dims), out_shape=jax.ShapeDtypeS...  27.7 us
    add x1, local copies, waits for them, and re-layouts, per_device(): out = out + share[:, None, None, None] * ext[1 + t][None]  1.25 us
    add x1, other arithmetic, per_device(): out = out + share[:, None, None, None] * ext[1 + t][None]  1.15 us

profile of v1, /device:TPU:24, one launch (start us, length us, event | category | flops | bytes accessed | tf_op | source)
XLA Modules:
  0.0 30.2 jit_solution(2283895219619981649)
XLA Ops:
  0.0 0.0 copy-start.1
  0.0 0.0 copy-start
  0.0 27.7 %shard_map.64 = f32[3,2,2,2,64,128]{5,4,3,2,1,0:T(8,128)} custom-call(f32[20,8,128]{2,1,0:T(8,128)} %bitcast.22, bf16[10,2,2,2,2,64,128]{6,5,4,3,2,1,0:T(8,128)(2,1)} %bitcast.21, f32[2,64]{1,0:T(2,128)} %bitcast.23, s32[4]{0:T(128)} %counts.1), custom_call_target="tpu_custom_call" | custom-call | tf_op jit(solution)/shard_map/pallas_call | solution.py:372
  27.8 1.2 %slice_bitcast_fusion.2 = (f32[64,4,256]{2,1,0:T(4,128)S(1)}, f32[64,4,256]{2,1,0:T(4,128)S(1)}, f32[64,4,256]{2,1,0:T(4,128)S(1)}) fusion(f32[3,64,4,2,128]{4,2,3,1,0:T(4,128)} %bitcast.20), kind=kLoop, calls=%fused_computation.3 | loop fusion | bytes 1572864 | tf_op jit(solution)/shard_map/add | solution.py:414
  29.0 0.0 copy-done.1
  29.0 0.0 copy-done
  29.0 1.2 %multiply_add_fusion = f32[3,64,4,256]{3,2,1,0:T(4,128)} fusion(f32[64,4,256]{2,1,0:T(4,128)S(1)} %get-tuple-element.6, f32[3]{0:T(128)S(1)} %get-tuple-element.9, f32[64,4,256]{2,1,0:T(4,128)S(1)} %get-tuple-element.7, f32[3]{0:T(128)S(1)} %get-tuple-element.8, f32[64,4,256]{2,1,0:T(4,128)S(1)} %get-tuple-element.5), kind=kLoop, calls=%fused_computation | loop fusion | flops 786432 | bytes 1572888 | tf_op jit(solution)/shard_map/add | solution.py:414
  (1 shorter events, 0.0 us)
Async XLA Ops:
  0.0 29.0 %copy-start.1 = (s32[3]{0:T(128)S(1)}, s32[3]{0:T(128)}, u32[]{:S(2)}) copy-start(s32[3]{0:T(128)} %param.10) | copy-start | bytes 40
  0.0 29.0 %copy-start = (f32[3]{0:T(128)S(1)}, f32[3]{0:T(128)}, u32[]{:S(2)}) copy-start(f32[3]{0:T(128)} %param.11) | copy-start | bytes 40

commit v2 on v1

--- a/solution.py
+++ b/solution.py
@@ -9,6 +9,8 @@
 from jax.sharding import PartitionSpec as P
 
 SMOOTH = 4
+CHUNKS = 4
+PIECES = 4
 LANES = 128
 MESH = pl.DeviceIdType.MESH
 
@@ -42,13 +44,13 @@
         order += [(0, outer_peer(e), inner_peer(d)) for e in range(1, outer + 1)]
     for e in range(1, outer):
         order += [(1, outer_peer(e), inner_peer(d)) for d in range(1, inner + 1)]
-    sent = len(order)
     order += [(0, outer_peer(e), ix) for e in range(1, outer + 1)]
     order += [(1, jy, inner_peer(d)) for d in range(1, inner + 1)]
     loads = []
-    for n, (p, j, i) in enumerate(order):
+    for n, (o, j, i) in enumerate(order):
+        span = pl.ds(o * CHUNKS, CHUNKS)
         copy = pltpu.make_async_copy(
-            perturbations.at[:, :, j, i, p], pert.at[:, :, j, i, p], pert_sem.at[n])
+            perturbations.at[:, :, j, i, span], pert.at[:, :, j, i, span], pert_sem.at[n])
         copy.start()
         loads.append(copy)
 
@@ -134,77 +136,86 @@
 
     pair = 2 * level_rows
 
-    def block(p, j, i):
-        base = ((j * inner + i) * 2 + p) * part_levels
-
-        def body(u, carry):
-            for t in range(slots):
-                acc = [[None] * 2 for _ in range(modes_n)]
-                for k in range(members):
-                    x = pert[k, t, j, i, p, pl.ds(pl.multiple_of(u * pair, pair), pair), :].astype(jnp.float32)
-                    for m in range(modes_n):
-                        s = smooth[k * modes_n + m]
-                        for v in range(2):
-                            term = s * x[v * level_rows:(v + 1) * level_rows]
-                            acc[m][v] = term if k == 0 else acc[m][v] + term
-                for v in range(2):
-                    total = modes[0, base + 2 * u + v] * acc[0][v]
-                    for m in range(1, modes_n):
-                        total = total + modes[m, base + 2 * u + v] * acc[m][v]
-                    part[p, t, j, i, pl.ds(pl.multiple_of(u * pair + v * level_rows, level_rows), level_rows), :] = total
+    def sums(p, j, i, u):
+        base = ((j * inner + i) * 2 * CHUNKS + p) * part_levels + 2 * u
+        for t in range(slots):
+            acc = [[None] * 2 for _ in range(modes_n)]
+            for k in range(members):
+                x = pert[k, t, j, i, p, pl.ds(pl.multiple_of(u * pair, pair), pair), :].astype(jnp.float32)
+                for m in range(modes_n):
+                    s = smooth[k * modes_n + m]
+                    for v in range(2):
+                        term = s * x[v * level_rows:(v + 1) * level_rows]
+                        acc[m][v] = term if k == 0 else acc[m][v] + term
+            for v in range(2):
+                total = modes[0, base + v] * acc[0][v]
+                for m in range(1, modes_n):
+                    total = total + modes[m, base + v] * acc[m][v]
+                part[p, t, j, i, pl.ds(pl.multiple_of(u * pair + v * level_rows, level_rows), level_rows), :] = total
+
+    pairs = rows // pair
+
+    def sums_over(count, place):
+        def body(n, carry):
+            u, n = n % pairs, n // pairs
+            sums(*place(n), u)
             return carry
 
-        lax.fori_loop(0, rows // pair, body, 0)
+        lax.fori_loop(0, count * pairs, body, 0)
 
     def remote(src, dst, send, recv, to):
         return pltpu.make_async_remote_copy(
             src_ref=src, dst_ref=dst, send_sem=send, recv_sem=recv, device_id=to, device_id_type=MESH)
 
     steps_in, steps_out = range(1, inner), range(1, outer)
-    n_in = inner - 1
-    rs1a = [remote(part.at[0, :, :, inner_peer(d)], first_a.at[d - 1],
-                   rs_send.at[0, d - 1], rs_recv.at[0, d - 1], at(jy, inner_peer(d))) for d in steps_in]
-    rs1b = [remote(part.at[1, :, outer_peer(e)], first_b.at[e - 1],
-                   rs_send.at[1, e - 1], rs_recv.at[1, e - 1], at(outer_peer(e), ix)) for e in steps_out]
-    rs2a = [remote(mid_a.at[e - 1], second_a.at[e - 1],
-                   rs_send.at[2, e - 1], rs_recv.at[2, e - 1], at(outer_peer(e), ix)) for e in steps_out]
-    rs2b = [remote(mid_b.at[d - 1], second_b.at[d - 1],
-                   rs_send.at[3, d - 1], rs_recv.at[3, d - 1], at(jy, inner_peer(d))) for d in steps_in]
-
-    n = 0
-    for copy in rs1a:
-        for _ in range(outer):
-            loads[n].wait()
-            block(*order[n])
-            n += 1
-        copy.start()
-    for copy in rs1b:
-        for _ in range(inner):
-            loads[n].wait()
-            block(*order[n])
-            n += 1
-        copy.start()
-    while n < len(order):
-        loads[n].wait()
-        block(*order[n])
-        n += 1
-
-    for copy in rs1a:
-        copy.wait_recv()
-    for e, copy in zip(steps_out, rs2a):
-        total = part[0, :, outer_peer(e), ix]
-        for d in steps_in:
-            total = total + first_a[d - 1, :, outer_peer(e)]
-        mid_a[e - 1] = total
-        copy.start()
-    for copy in rs1b:
-        copy.wait_recv()
-    for d, copy in zip(steps_in, rs2b):
-        total = part[1, :, jy, inner_peer(d)]
-        for e in steps_out:
-            total = total + first_b[e - 1, :, inner_peer(d)]
-        mid_b[d - 1] = total
-        copy.start()
+    rs1, rs2 = [[], []], [[], []]
+    for c in range(CHUNKS):
+        pa, pb = c, CHUNKS + c
+        rs1[0].append([remote(part.at[pa, :, :, inner_peer(d)], first_a.at[c, d - 1],
+                              rs_send.at[0, c, d - 1], rs_recv.at[0, c, d - 1], at(jy, inner_peer(d)))
+                       for d in steps_in])
+        rs1[1].append([remote(part.at[pb, :, outer_peer(e)], first_b.at[c, e - 1],
+                              rs_send.at[1, c, e - 1], rs_recv.at[1, c, e - 1], at(outer_peer(e), ix))
+                       for e in steps_out])
+        rs2[0].append([remote(mid_a.at[c, e - 1], second_a.at[c, e - 1],
+                              rs_send.at[2, c, e - 1], rs_recv.at[2, c, e - 1], at(outer_peer(e), ix))
+                       for e in steps_out])
+        rs2[1].append([remote(mid_b.at[c, d - 1], second_b.at[c, d - 1],
+                              rs_send.at[3, c, d - 1], rs_recv.at[3, c, d - 1], at(jy, inner_peer(d)))
+                       for d in steps_in])
+
+    n_first = (inner - 1) * outer + (outer - 1) * inner
+    for copy in loads[:n_first]:
+        copy.wait()
+    for c in range(CHUNKS):
+        for d, copy in zip(steps_in, rs1[0][c]):
+            sums_over(outer, lambda n: (c, outer_peer(n), inner_peer(d)))
+            copy.start()
+        for e, copy in zip(steps_out, rs1[1][c]):
+            sums_over(inner, lambda n: (CHUNKS + c, outer_peer(e), inner_peer(n)))
+            copy.start()
+    for copy in loads[n_first:]:
+        copy.wait()
+    sums_over(CHUNKS * outer, lambda n: (n // outer, n % outer, ix))
+    sums_over(CHUNKS * inner, lambda n: (CHUNKS + n // inner, jy, n % inner))
+
+    for c in range(CHUNKS):
+        for copy in rs1[0][c]:
+            copy.wait_recv()
+        for e, copy in zip(steps_out, rs2[0][c]):
+            total = part[c, :, outer_peer(e), ix]
+            for d in steps_in:
+                total = total + first_a[c, d - 1, :, outer_peer(e)]
+            mid_a[c, e - 1] = total
+            copy.start()
+        for copy in rs1[1][c]:
+            copy.wait_recv()
+        for d, copy in zip(steps_in, rs2[1][c]):
+            total = part[CHUNKS + c, :, jy, inner_peer(d)]
+            for e in steps_out:
+                total = total + first_b[c, e - 1, :, inner_peer(d)]
+            mid_b[c, d - 1] = total
+            copy.start()
 
     def gathers(unit, row0, p):
         sends, relays = [], []
@@ -220,7 +231,7 @@
         for e in steps_out:
             sends.append(("out", e, move(jy, ix, at(outer_peer(e), ix), sem)))
             sem += 1
-        if p == 0:
+        if p < CHUNKS:
             for d in steps_in:
                 for e in steps_out:
                     relays.append((d, move(jy, inner_peer(inner - d), at(outer_peer(e), ix), sem)))
@@ -232,15 +243,17 @@
                     sem += 1
         return sends, relays
 
-    slot_gathers = [gathers(1, 0, p) for p in range(2)]
-    early_gathers = [gathers(0, 1, p) for p in range(2)]
+    parts = range(2 * CHUNKS)
+    turn = [o * CHUNKS + c for c in range(CHUNKS) for o in range(2)]
+    slot_gathers = [gathers(1, 0, p) for p in parts]
+    early_gathers = [gathers(0, 1, p) for p in parts]
 
     def start_gather(g):
         for _, _, copy in g[0]:
             copy.start()
 
     def relay_gather(g, p):
-        kind = "in" if p == 0 else "out"
+        kind = "in" if p < CHUNKS else "out"
         for name, d, copy in g[0]:
             if name == kind:
                 copy.wait_recv()
@@ -249,7 +262,7 @@
                         forward.start()
 
     def finish_gather(g, p):
-        kind = "in" if p == 0 else "out"
+        kind = "in" if p < CHUNKS else "out"
         for name, _, copy in g[0]:
             if name != kind:
                 copy.wait_recv()
@@ -261,7 +274,7 @@
             forward.wait_send()
 
     chain = [remote(passing.at[p], ext.at[0, jy, ix, p], z_send.at[p], z_recv.at[p], {"tm": tm + 1})
-             for p in range(2)]
+             for p in parts]
 
     def add_slots(p):
         total = ext[1, jy, ix, p]
@@ -270,25 +283,25 @@
         return total
 
     def own_total(p):
-        if p == 0:
-            total = part[0, :, jy, ix]
+        c = p % CHUNKS
+        total = part[p, :, jy, ix]
+        if p < CHUNKS:
             for d in steps_in:
-                total = total + first_a[d - 1, :, jy]
-            for copy in rs2a:
+                total = total + first_a[c, d - 1, :, jy]
+            for copy in rs2[0][c]:
                 copy.wait_recv()
             for e in steps_out:
-                total = total + second_a[e - 1]
+                total = total + second_a[c, e - 1]
         else:
-            total = part[1, :, jy, ix]
             for e in steps_out:
-                total = total + first_b[e - 1, :, ix]
-            for copy in rs2b:
+                total = total + first_b[c, e - 1, :, ix]
+            for copy in rs2[1][c]:
                 copy.wait_recv()
             for d in steps_in:
-                total = total + second_b[d - 1]
+                total = total + second_b[c, d - 1]
         ext[pl.ds(1, slots), jy, ix, p] = total
 
-    for p in range(2):
+    for p in turn:
         own_total(p)
 
         @pl.when(tm == 0)
@@ -300,47 +313,70 @@
 
         start_gather(slot_gathers[p])
 
-    def earlier():
-        for p in range(2):
-            @pl.when(tm > 0)
+    def earlier(p):
+        @pl.when(tm > 0)
+        def _():
+            chain[p].wait_recv()
+
+            @pl.when(tm < steps_tm - 1)
             def _():
-                chain[p].wait_recv()
-
-                @pl.when(tm < steps_tm - 1)
-                def _():
-                    passing[p] = ext[0, jy, ix, p] + add_slots(p)
-                    chain[p].start()
-
-            start_gather(early_gathers[p])
-
-    def relays():
-        for p in range(2):
+                passing[p] = ext[0, jy, ix, p] + add_slots(p)
+                chain[p].start()
+
+        start_gather(early_gathers[p])
+
+    @pl.when(tm == 1)
+    def _():
+        for p in turn:
+            earlier(p)
             relay_gather(slot_gathers[p], p)
 
-    @pl.when(tm <= 1)
+    @pl.when(tm != 1)
     def _():
-        earlier()
-        relays()
-
-    @pl.when(tm > 1)
-    def _():
-        relays()
-        earlier()
-
-    for p in range(2):
+        for p in turn:
+            relay_gather(slot_gathers[p], p)
+        for p in turn:
+            earlier(p)
+
+    for p in turn:
         relay_gather(early_gathers[p], p)
-    for p in range(2):
+    for p in turn:
         finish_gather(slot_gathers[p], p)
-    for p in range(2):
+    for p in turn:
         finish_gather(early_gathers[p], p)
 
     @pl.when(tm < steps_tm - 1)
     def _():
-        for p in range(2):
+        for p in parts:
             chain[p].wait_send()
 
-    for copy in halos + rs1a + rs1b + rs2a + rs2b:
+    for copy in halos:
         copy.wait_send()
+    for group in rs1 + rs2:
+        for copies in group:
+            for copy in copies:
+                copy.wait_send()
+
+
+def blend(slots, ext, index, weight, out, held, sems):
+    windows, total_rows, _ = out.shape
+    size = total_rows // PIECES
+    local = [index[w] - lax.axis_index("tm") * slots for w in range(windows)]
+    shares = [[jnp.where(local[w] > t, 1.0, jnp.where(local[w] == t, weight[w], 0.0))
+               for t in range(slots)] for w in range(windows)]
+    copies = []
+    for n in range(PIECES):
+        span = pl.ds(n * size, size)
+        for w in range(windows):
+            total = ext[0, span]
+            for t in range(slots):
+                total = total + shares[w][t] * ext[1 + t, span]
+            held[w, span] = total
+        copy = pltpu.make_async_copy(held.at[:, span], out.at[:, span], sems.at[n])
+        copy.start()
+        copies.append(copy)
+    for copy in copies:
+        copy.wait()
 
 
 def rows_view(x, nx, gy):
@@ -358,12 +394,13 @@
     tiles, n_mem, steps_tm = lax.axis_size("tile"), lax.axis_size("mem"), lax.axis_size("tm")
     inner = 2 if n_mem % 2 == 0 else 1
     outer = n_mem // inner
-    rows = levels // (n_mem * 2) * level_rows
+    parts = 2 * CHUNKS
+    rows = levels // (n_mem * parts) * level_rows
     assert nx >= SMOOTH and level_rows == 8 and rows % 16 == 0
     norm = 1.0 / math.sqrt(members * n_mem - 1)
     fields = members * modes_n
     c = rows_view(control, nx, gy).reshape(fields, level_rows, LANES)
-    q = rows_view(perturbations, nx, gy).reshape(members, slots, outer, inner, 2, rows, LANES)
+    q = rows_view(perturbations, nx, gy).reshape(members, slots, outer, inner, parts, rows, LANES)
     dims = (members, slots, modes_n, nx, halves, outer, inner, rows, tiles, steps_tm, norm)
     f32 = jnp.float32
     n_in, n_out = max(inner - 1, 1), max(outer - 1, 1)
@@ -371,10 +408,10 @@
     dma = pltpu.SemaphoreType.DMA
     ext = pl.pallas_call(
         functools.partial(kernel, dims),
-        out_shape=jax.ShapeDtypeStruct((slots + 1, outer, inner, 2, rows, LANES), f32),
+        out_shape=pltpu.VMEM((slots + 1, outer, inner, parts, rows, LANES), f32),
         in_specs=[
-            pl.BlockSpec(memory_space=pl.ANY),
-            pl.BlockSpec(memory_space=pl.ANY),
+            pl.BlockSpec(memory_space=pltpu.HBM),
+            pl.BlockSpec(memory_space=pltpu.HBM),
             pl.BlockSpec(memory_space=pltpu.SMEM),
             pl.BlockSpec(memory_space=pltpu.SMEM),
         ],
@@ -384,35 +421,44 @@
             pltpu.VMEM((2, fields, level_rows, LANES), f32),
             pltpu.VMEM(q.shape, q.dtype),
             pltpu.VMEM((fields, level_rows, LANES), f32),
-            pltpu.VMEM((2, slots, outer, inner, rows, LANES), f32),
-            pltpu.VMEM((n_in, slots, outer, rows, LANES), f32),
-            pltpu.VMEM((n_out, slots, inner, rows, LANES), f32),
-            pltpu.VMEM((n_out, slots, rows, LANES), f32),
-            pltpu.VMEM((n_in, slots, rows, LANES), f32),
-            pltpu.VMEM((n_out, slots, rows, LANES), f32),
-            pltpu.VMEM((n_in, slots, rows, LANES), f32),
-            pltpu.VMEM((2, rows, LANES), f32),
+            pltpu.VMEM((parts, slots, outer, inner, rows, LANES), f32),
+            pltpu.VMEM((CHUNKS, n_in, slots, outer, rows, LANES), f32),
+            pltpu.VMEM((CHUNKS, n_out, slots, inner, rows, LANES), f32),
+            pltpu.VMEM((CHUNKS, n_out, slots, rows, LANES), f32),
+            pltpu.VMEM((CHUNKS, n_in, slots, rows, LANES), f32),
+            pltpu.VMEM((CHUNKS, n_out, slots, rows, LANES), f32),
+            pltpu.VMEM((CHUNKS, n_in, slots, rows, LANES), f32),
+            pltpu.VMEM((parts, rows, LANES), f32),
             dma,
             dma((2 * n_mem,)),
             dma((2,)),
             dma((2,)),
-            dma((4, max(n_in, n_out))),
-            dma((4, max(n_in, n_out))),
-            dma((2,)),
-            dma((2,)),
-            dma((2, 2, n_gather)),
-            dma((2, 2, n_gather)),
+            dma((4, CHUNKS, max(n_in, n_out))),
+            dma((4, CHUNKS, max(n_in, n_out))),
+            dma((parts,)),
+            dma((parts,)),
+            dma((2, parts, n_gather)),
+            dma((2, parts, n_gather)),
         ],
-        compiler_params=pltpu.CompilerParams(collective_id=0, has_side_effects=True),
+        compiler_params=pltpu.CompilerParams(
+            collective_id=0, has_side_effects=True),
     )(c, q, vertical_modes.T, mode_counts)
-    ext = ext.reshape(slots + 1, levels, halves, nx, LANES)
-    ext = jnp.swapaxes(ext, 2, 3).reshape(slots + 1, levels, nx, gy)
-    local = slot_index - lax.axis_index("tm") * slots
-    out = ext[0][None]
-    for t in range(slots):
-        share = jnp.where(local > t, 1.0, jnp.where(local == t, blend_weight, 0.0))
-        out = out + share[:, None, None, None] * ext[1 + t][None]
-    return out
+    ext = ext.reshape(slots + 1, levels * level_rows, LANES)
+    windows = slot_index.shape[0]
+    out = pl.pallas_call(
+        functools.partial(blend, slots),
+        out_shape=jax.ShapeDtypeStruct((windows, levels * level_rows, LANES), f32),
+        in_specs=[
+            pl.BlockSpec(memory_space=pltpu.VMEM),
+            pl.BlockSpec(memory_space=pltpu.SMEM),
+            pl.BlockSpec(memory_space=pltpu.SMEM),
+        ],
+        out_specs=pl.BlockSpec(memory_space=pltpu.HBM),
+        scratch_shapes=[pltpu.VMEM((windows, levels * level_rows, LANES), f32), dma((PIECES,))],
+        compiler_params=pltpu.CompilerParams(vmem_limit_bytes=8 << 20),
+    )(ext, slot_index, blend_weight)
+    out = out.reshape(windows, levels, halves, nx, LANES)
+    return jnp.swapaxes(out, 2, 3).reshape(windows, levels, nx, gy)
 
 
 def solution(mesh):

time: 30.4 us -> 27.6 us (0.908)
  local copies, waits for them, and re-layouts: 1.25 us -> 0.01 us
  other arithmetic: 1.16 us -> 0 us
    add x1 -> x0, local copies, waits for them, and re-layouts: 1.25 us -> none  [per_device(): out = out + share[:, None, None, None] * ext[1 + t][None]]
    add x1 -> x0, other arithmetic: 1.15 us -> none  [per_device(): out = out + share[:, None, None, None] * ext[1 + t][None]]
    pallas_call x1 -> x2, Pallas kernels: 27.7 us -> 27.4 us  [the longest x1 25.9 us: per_device(): pl.pallas_call(functools.partial(kernel, dims), out_shape=pltpu.VMEM((slo...]
where the time goes in v2:
time: 27.6 us; the launch traced here: 27.4 us
  Pallas kernels  27.4 us (99%)
    pallas_call x1, Pallas kernels, per_device(): pl.pallas_call(functools.partial(kernel, dims), out_shape=pltpu.VMEM((slo...  25.9 us
    pallas_call x1, Pallas kernels, per_device(): pl.pallas_call(functools.partial(blend, slots), out_shape=jax.ShapeDtypeS...  1.49 us

profile of v2, /device:TPU:24, one launch (start us, length us, event | category | flops | bytes accessed | tf_op | source)
XLA Modules:
  0.0 27.4 jit_solution(12877802114026739741)
XLA Ops:
  0.0 0.0 copy-start.1
  0.0 0.0 copy-start
  0.0 25.9 %shard_map.64 = f32[3,2,2,8,16,128]{5,4,3,2,1,0:T(8,128)S(1)} custom-call(f32[20,8,128]{2,1,0:T(8,128)} %bitcast.19, bf16[10,2,2,2,8,16,128]{6,5,4,3,2,1,0:T(8,128)(2,1)} %bitcast.18, f32[2,64]{1,0:T(2,128)} %bitcast.20, s32[4]{0:T(128)} %counts.1), custom_call_target="tpu_custom_call" | custom-call | tf_op jit(solution)/shard_map/pallas_call | solution.py:409
  25.9 0.0 copy-done.1
  25.9 0.0 copy-done
  26.0 1.5 %shard_map.65 = f32[3,512,128]{2,1,0:T(8,128)} custom-call(f32[3,512,128]{2,1,0:T(8,128)S(1)} %bitcast.17, s32[3]{0:T(128)S(1)} %copy-done, f32[3]{0:T(128)S(1)} %copy-done.1), custom_call_target="tpu_custom_call" | custom-call | tf_op jit(solution)/shard_map/pallas_call | solution.py:448
Async XLA Ops:
  0.0 25.9 %copy-start.1 = (f32[3]{0:T(128)S(1)}, f32[3]{0:T(128)}, u32[]{:S(2)}) copy-start(f32[3]{0:T(128)} %weight.1) | copy-start | bytes 40
  0.0 25.9 %copy-start = (s32[3]{0:T(128)S(1)}, s32[3]{0:T(128)}, u32[]{:S(2)}) copy-start(s32[3]{0:T(128)} %index.1) | copy-start | bytes 40

commit v3 on v2

--- a/solution.py
+++ b/solution.py
@@ -10,6 +10,7 @@
 
 SMOOTH = 4
 CHUNKS = 4
+DIRECT = (1,)
 PIECES = 4
 LANES = 128
 MESH = pl.DeviceIdType.MESH
@@ -56,13 +57,14 @@
 
     barrier = pltpu.get_barrier_semaphore()
     tile_offsets = sorted({1 % tiles, (tiles - 1) % tiles} - {0})
-    expected = len(tile_offsets) + (inner - 1) + (outer - 1)
+    expected = len(tile_offsets) + inner * outer - 1
     for d in tile_offsets:
         pl.semaphore_signal(barrier, inc=1, device_id={"tile": (tile + d) % tiles}, device_id_type=MESH)
     for d in range(1, inner):
         pl.semaphore_signal(barrier, inc=1, device_id=at(jy, inner_peer(d)), device_id_type=MESH)
     for e in range(1, outer):
-        pl.semaphore_signal(barrier, inc=1, device_id=at(outer_peer(e), ix), device_id_type=MESH)
+        for d in range(inner):
+            pl.semaphore_signal(barrier, inc=1, device_id=at(outer_peer(e), inner_peer(d)), device_id_type=MESH)
 
     @pl.when(tm > 0)
     def _():
@@ -231,7 +233,12 @@
         for e in steps_out:
             sends.append(("out", e, move(jy, ix, at(outer_peer(e), ix), sem)))
             sem += 1
-        if p < CHUNKS:
+        if row0 in DIRECT:
+            for d in steps_in:
+                for e in steps_out:
+                    sends.append(("diagonal", d, move(jy, ix, at(outer_peer(e), inner_peer(d)), sem)))
+                    sem += 1
+        elif p < CHUNKS:
             for d in steps_in:
                 for e in steps_out:
                     relays.append((d, move(jy, inner_peer(inner - d), at(outer_peer(e), ix), sem)))

time: 27.6 us -> 25.5 us (0.924)
  Pallas kernels: 27.4 us -> 25.3 us
    pallas_call x1, Pallas kernels: 25.9 us -> 23.8 us  [per_device(): pl.pallas_call(functools.partial(kernel, dims), out_shape=pltpu.VMEM((slo...]
where the time goes in v3:
time: 25.5 us; the launch traced here: 25.3 us
  Pallas kernels  25.3 us (99%)
    pallas_call x1, Pallas kernels, per_device(): pl.pallas_call(functools.partial(kernel, dims), out_shape=pltpu.VMEM((slo...  23.8 us
    pallas_call x1, Pallas kernels, per_device(): pl.pallas_call(functools.partial(blend, slots), out_shape=jax.ShapeDtypeS...  1.49 us

profile of v3, /device:TPU:24, one launch (start us, length us, event | category | flops | bytes accessed | tf_op | source)
XLA Modules:
  0.0 25.3 jit_solution(4726012480319957877)
XLA Ops:
  0.0 0.0 copy-start.1
  0.0 0.0 copy-start
  0.0 23.8 %shard_map.64 = f32[3,2,2,8,16,128]{5,4,3,2,1,0:T(8,128)S(1)} custom-call(f32[20,8,128]{2,1,0:T(8,128)} %bitcast.19, bf16[10,2,2,2,8,16,128]{6,5,4,3,2,1,0:T(8,128)(2,1)} %bitcast.18, f32[2,64]{1,0:T(2,128)} %bitcast.20, s32[4]{0:T(128)} %counts.1), custom_call_target="tpu_custom_call" | custom-call | tf_op jit(solution)/shard_map/pallas_call | solution.py:416
  23.8 0.0 copy-done.1
  23.8 0.0 copy-done
  23.9 1.5 %shard_map.65 = f32[3,512,128]{2,1,0:T(8,128)} custom-call(f32[3,512,128]{2,1,0:T(8,128)S(1)} %bitcast.17, s32[3]{0:T(128)S(1)} %copy-done, f32[3]{0:T(128)S(1)} %copy-done.1), custom_call_target="tpu_custom_call" | custom-call | tf_op jit(solution)/shard_map/pallas_call | solution.py:455
Async XLA Ops:
  0.0 23.8 %copy-start.1 = (f32[3]{0:T(128)S(1)}, f32[3]{0:T(128)}, u32[]{:S(2)}) copy-start(f32[3]{0:T(128)} %weight.1) | copy-start | bytes 40
  0.0 23.8 %copy-start = (s32[3]{0:T(128)S(1)}, s32[3]{0:T(128)}, u32[]{:S(2)}) copy-start(s32[3]{0:T(128)} %index.1) | copy-start | bytes 40
